TPU v7x, 256 devices: a whole 4x4x8 slice. The times are simulated.
256 devices in a mesh: slab: 64 (over z, x, core), grp: 4 (over y).
Axes of the slice: x: 4, y: 4, z: 8, core: 2. Of those that a mesh axis runs over, the one named last changes fastest.
Arguments:
- iterate: float32 [24576, 256], P(('slab', 'grp')), may hold values from -6 to 6
- residual: float32 [24576, 256], P(('slab', 'grp')), may hold values from -6 to 6
- direction: float32 [24576, 256], P(('slab', 'grp')), may hold values from -6 to 6
- prior_rho: float32 [256], replicated, may hold values from 12288 to 49152
- diag_blocks: float32 [24576, 384], P(('slab', 'grp')), as said below
- lower_coupling: float32 [24576, 128], P(('slab', 'grp')), may hold values from -0.125 to 0.125
- upper_coupling: float32 [24576, 128], P(('slab', 'grp')), may hold values from -0.125 to 0.125
- interface: int32 [64, 128], P('slab'), may hold values from 0 to 383, as said below
- jacobi_inverse: float32 [24576, 96], P(('slab', 'grp'))
- slab_inverse: float32 [24576, 384], P(('slab', 'grp'))
- lower_factor: float32 [24576, 128], P(('slab', 'grp')), may hold values from -0.875 to 0.875
- upper_factor: float32 [24576, 128], P(('slab', 'grp')), may hold values from -0.5 to 0.5
Outputs:
- new_iterate: float32 [24576, 256], P(('slab', 'grp'))
- new_residual: float32 [24576, 256], P(('slab', 'grp'))
- new_direction: float32 [24576, 256], P(('slab', 'grp'))
- new_rho: float32 [256], replicated
Inputs may be any that keep to these rules, and one draw needn't show every extreme that they name: `interface`: row k lists 128 distinct dof numbers of slab k. `diag_blocks`: each diagonal block is a positive diagonal plus a skew-symmetric part.
All inputs are finite; a program needn't handle non-finite values.
Results may differ from a plain program's by a relative error of at most 0.0003.
Values sent between devices are 32-bit elements; how exact they have to be, the bound alone decides.
No kernel may reach another device: no remote copies, remote signals or barrier semaphores. Data moves between devices by JAX's collectives and lax.ppermute only.
A program may use at most 64 MiB of HBM per device.

v0:
```python
import functools

import jax
import jax.numpy as jnp
from jax import lax
from jax.sharding import Mesh
from jax.sharding import PartitionSpec as P

SLAB = ("slab_0", "slab_1", "slab_2")
SLAB_GRP = ("slab_0", "slab_1", "slab_2", "grp")


def in_order(pieces, dim):
    dims = list(pieces.shape[1:])
    dims[dim] *= pieces.shape[0]
    return jnp.moveaxis(pieces, 0, dim).reshape(dims)


def sent_to_all(x, axis):
    copies = jnp.broadcast_to(x, (lax.axis_size(axis), *x.shape))
    return lax.all_to_all(copies, axis, split_axis=0, concat_axis=0, tiled=True)


def gathered_copies(x, axis, dim):
    return in_order(sent_to_all(x, axis), dim)


def extended(cells, sides, width):
    for axis, dim in sides:
        count = lax.axis_size(axis)
        ends = count - 1
        head = lax.slice_in_dim(cells, 0, width, axis=dim)
        tail = lax.slice_in_dim(cells, cells.shape[dim] - width, cells.shape[dim], axis=dim)
        cells = jnp.concatenate(
            [
                lax.ppermute(tail, axis, [(i, (i + 1) % count) for i in range(ends)]),
                cells,
                lax.ppermute(head, axis, [((i + 1) % count, i) for i in range(ends)]),
            ],
            axis=dim,
        )
    return cells


def by_axis(x, axes):
    return functools.reduce(lax.psum, axes, x)


def sent_together(arrays, axis, dim, along):
    both = jnp.concatenate(arrays, axis=along)
    result, at, done = (lax.all_gather(both, axis, axis=dim, tiled=True), 0, [])
    for a in arrays:
        done.append(lax.slice_in_dim(result, at, at + a.shape[along], axis=along))
        at += a.shape[along]
    return tuple(done)


def filled_with(x, identity):
    return jax.tree.map(
        lambda part, zero: jnp.zeros_like(part) + jnp.asarray(zero, part.dtype), x, identity
    )


def entering(x, axes, combine, identity, reverse):
    before = start = filled_with(x, identity)
    subtotal = x
    for axis in reversed(axes):
        length, position = (lax.axis_size(axis), lax.axis_index(axis))
        pieces = jax.tree.map(lambda part: lax.all_gather(part, axis), subtotal)
        inside, subtotal = (start, start)
        for k in reversed(range(length)) if reverse else range(length):
            passed = k > position if reverse else k < position
            subtotal = combine(subtotal, jax.tree.map(lambda part: part[k], pieces))
            inside = jax.tree.map(lambda new, old: jnp.where(passed, new, old), subtotal, inside)
        before = combine(inside, before)
    return before


def matmul(left, right):
    return jnp.dot(left, right, precision=lax.Precision.HIGHEST, preferred_element_type=jnp.float32)


def compose(earlier, later):
    return (matmul(later[0], earlier[0]), matmul(later[0], earlier[1]) + later[1])


def local(
    iterate,
    residual,
    direction,
    prior_rho,
    diag_blocks,
    lower_coupling,
    upper_coupling,
    interface,
    jacobi_inverse,
    slab_inverse,
    lower_factor,
    upper_factor,
):
    index_rows = interface[0]

    def operate(field):
        gathered = gathered_copies(field, "grp", 0)
        faces = gathered[index_rows]
        beside_all = extended(faces[None], ((SLAB, 0),), 1)
        return (
            matmul(diag_blocks, gathered)
            + matmul(lower_coupling, beside_all[0])
            + matmul(upper_coupling, beside_all[2])
        )

    image = operate(direction)
    curvature = by_axis(jnp.sum(direction * image, axis=0), SLAB_GRP)
    step_size = prior_rho / curvature
    new_iterate = iterate + step_size * direction
    new_residual = residual - step_size * image
    smoothed = matmul(jacobi_inverse, new_residual)
    defect = new_residual - operate(smoothed)
    defect_full, lower_full, upper_full = sent_together(
        (defect, lower_factor, upper_factor), "grp", 0, 1
    )
    solved = matmul(slab_inverse, defect_full)
    factor_rows = matmul(slab_inverse, lower_full)
    solved_full, factor_full = sent_together((solved, factor_rows), "grp", 0, 1)
    offsets = solved_full[index_rows]
    transfer = -factor_full[index_rows]
    upper_iface = -upper_full[index_rows]
    identity_map = jnp.eye(transfer.shape[0], dtype=jnp.float32)
    forward_map = entering(
        (transfer, offsets), SLAB, compose, (identity_map, jnp.zeros_like(offsets)), False
    )
    forward_prev = forward_map[1]
    forward_vals = solved - matmul(factor_rows, forward_prev)
    iface_vals = offsets + matmul(transfer, forward_prev)
    backward_map = entering(
        (upper_iface, iface_vals), SLAB, compose, (identity_map, jnp.zeros_like(iface_vals)), True
    )
    backward_next = backward_map[1]
    correction = forward_vals - matmul(upper_factor, backward_next)
    precond = smoothed + correction
    new_rho = by_axis(jnp.sum(new_residual * precond, axis=0), SLAB_GRP)
    new_direction = precond + new_rho / prior_rho * direction
    return (new_iterate, new_residual, new_direction, new_rho)


def solution(mesh):
    split = Mesh(
        mesh.devices.reshape(8, 4, 2, mesh.shape["grp"]), ("slab_0", "slab_1", "slab_2", "grp")
    )
    placed = (
        P(SLAB_GRP, None),
        P(SLAB_GRP, None),
        P(SLAB_GRP, None),
        P(),
        P(SLAB_GRP, None),
        P(SLAB_GRP, None),
        P(SLAB_GRP, None),
        P(SLAB, None),
        P(SLAB_GRP, None),
        P(SLAB_GRP, None),
        P(SLAB_GRP, None),
        P(SLAB_GRP, None),
    )
    return jax.shard_map(
        local,
        mesh=split,
        in_specs=placed,
        out_specs=(P(SLAB_GRP, None), P(SLAB_GRP, None), P(SLAB_GRP, None), P()),
        check_vma=False,
    )
```

profile of v0, /device:TPU:1, one launch (start us, length us, event | category | flops | bytes accessed | tf_op | source)
XLA Modules:
  0.0 314.1 jit_solution(16572585691462652370)
XLA Ops:
  7.2 1.7 broadcast_in_dim.8
  8.9 5.1 %all-to-all-start = ((f32[4,96,256]{2,1,0:T(8,128)}), f32[4,96,256]{2,1,0:T(8,128)S(1)}, u32[]{:S(2)}, u32[]{:S(2)}) async-start(f32[4,96,256]{2,1,0:T(8,128)} %broadcast_in_dim.8), calls=%async_computation | async-start | bytes 786432 | tf_op jit(solution)/shard_map/all_to_all | solution.py:21
  14.0 6.2 %all-to-all-done = f32[4,96,256]{2,1,0:T(8,128)S(1)} async-done(((f32[4,96,256]{2,1,0:T(8,128)}), f32[4,96,256]{2,1,0:T(8,128)S(1)}, u32[]{:S(2)}, u32[]{:S(2)}) %all-to-all-start) | async-done | bytes 393248 | tf_op jit(solution)/shard_map/all_to_all | solution.py:21
  20.3 0.8 gather_fusion
  21.1 5.9 %collective-permute-start = (f32[1,128,256]{2,1,0:T(8,128)S(1)}, f32[1,128,256]{2,1,0:T(8,128)S(1)}, u32[]{:S(2)}, u32[]{:S(2)}) collective-permute-start(f32[1,128,256]{2,1,0:T(8,128)S(1)} %bitcast.105), channel_id=1, source_target_pairs={{0,4},{4,8},{8,12},{12,16},{16,20},{20,24},{24,28},{28,32},{32,36}... | collective-permute-start | bytes 393224 | tf_op jit(solution)/shard_map/ppermute | solution.py:36
  27.0 1.9 collective-permute-start.1
  28.9 0.4 fusion.143
  29.6 3.7 %collective-permute-done.1 = f32[1,128,256]{2,1,0:T(8,128)S(1)} collective-permute-done((f32[1,128,256]{2,1,0:T(8,128)S(1)}, f32[1,128,256]{2,1,0:T(8,128)S(1)}, u32[]{:S(2)}, u32[]{:S(2)}) %collective-permute-start.1) | collective-permute-done | bytes 131104 | tf_op jit(solution)/shard_map/ppermute | solution.py:38
  33.5 16.2 %psum.56 = f32[256]{0:T(256)S(1)} all-reduce(f32[256]{0:T(256)S(1)} %get-tuple-element.6), channel_id=1, replica_groups=mesh['slab_0'=8,'slab_1'=4,'slab_2'=2,'grp'=4] {'slab_0'}, use_global_device_ids=true, to_apply=%region_1.0 | all-reduce | flops 256 | bytes 2048 | tf_op jit(solution)/shard_map/psum | solution.py:46
  49.8 10.4 %psum.57 = f32[256]{0:T(256)S(1)} all-reduce(f32[256]{0:T(256)S(1)} %psum.56), channel_id=1, replica_groups=mesh['slab_0'=8,'slab_1'=4,'slab_2'=2,'grp'=4] {'slab_1'}, use_global_device_ids=true, to_apply=%region_2.0 | all-reduce | flops 256 | bytes 2048 | tf_op jit(solution)/shard_map/psum | solution.py:46
  60.1 4.7 %psum.58 = f32[256]{0:T(256)S(1)} all-reduce(f32[256]{0:T(256)S(1)} %psum.57), channel_id=1, replica_groups=mesh['slab_0'=8,'slab_1'=4,'slab_2'=2,'grp'=4] {'slab_2'}, use_global_device_ids=true, to_apply=%region_3.0 | all-reduce | flops 256 | bytes 2048 | tf_op jit(solution)/shard_map/psum | solution.py:46
  64.9 7.0 %psum.59 = f32[256]{0:T(256)S(1)} all-reduce(f32[256]{0:T(256)S(1)} %psum.58), channel_id=1, replica_groups=mesh['slab_0'=8,'slab_1'=4,'slab_2'=2,'grp'=4] {'grp'}, use_global_device_ids=true, to_apply=%region_4.0 | all-reduce | flops 256 | bytes 2048 | tf_op jit(solution)/shard_map/psum | solution.py:46
  71.9 0.8 copy-done.16
  72.9 0.8 broadcast_in_dim.10
  73.7 3.5 %all-to-all-start.1 = ((f32[4,96,256]{2,1,0:T(8,128)}), f32[4,96,256]{2,1,0:T(8,128)S(1)}, u32[]{:S(2)}, u32[]{:S(2)}) async-start(f32[4,96,256]{2,1,0:T(8,128)} %broadcast_in_dim.10), calls=%async_computation.1 | async-start | bytes 786432 | tf_op jit(solution)/shard_map/all_to_all | solution.py:21
  77.3 6.1 %all-to-all-done.1 = f32[4,96,256]{2,1,0:T(8,128)S(1)} async-done(((f32[4,96,256]{2,1,0:T(8,128)}), f32[4,96,256]{2,1,0:T(8,128)S(1)}, u32[]{:S(2)}, u32[]{:S(2)}) %all-to-all-start.1) | async-done | bytes 393248 | tf_op jit(solution)/shard_map/all_to_all | solution.py:21
  83.4 0.8 gather_fusion.1
  84.1 6.4 %collective-permute-start.2 = (f32[1,128,256]{2,1,0:T(8,128)S(1)}, f32[1,128,256]{2,1,0:T(8,128)S(1)}, u32[]{:S(2)}, u32[]{:S(2)}) collective-permute-start(f32[1,128,256]{2,1,0:T(8,128)S(1)} %bitcast.107), channel_id=1, source_target_pairs={{0,4},{4,8},{8,12},{12,16},{16,20},{20,24},{24,28},{28,32},{32,36}... | collective-permute-start | bytes 393224 | tf_op jit(solution)/shard_map/ppermute | solution.py:36
  90.5 1.9 collective-permute-start.3
  92.5 0.4 fusion.144
  93.1 3.7 %collective-permute-done.3 = f32[1,128,256]{2,1,0:T(8,128)S(1)} collective-permute-done((f32[1,128,256]{2,1,0:T(8,128)S(1)}, f32[1,128,256]{2,1,0:T(8,128)S(1)}, u32[]{:S(2)}, u32[]{:S(2)}) %collective-permute-start.3) | collective-permute-done | bytes 131104 | tf_op jit(solution)/shard_map/ppermute | solution.py:38
  97.1 11.6 %all_gather.74 = f32[384,512]{1,0:T(8,128)S(1)} all-gather(f32[96,512]{1,0:T(8,128)S(1)} %pad_maximum_fusion), channel_id=1, replica_groups=mesh['slab_0'=8,'slab_1'=4,'slab_2'=2,'grp'=4] {'grp'}, dimensions={0}, use_global_device_ids=true | all-gather | bytes 983040 | tf_op jit(solution)/shard_map/all_gather | solution.py:51
  108.7 0.4 convolution_bitcast_fusion.4
  109.1 0.3 fusion.9
  109.5 12.0 %all_gather.75 = f32[384,384]{1,0:T(8,128)S(1)} all-gather(f32[96,384]{1,0:T(8,128)S(1)} %pad_maximum_fusion.1), channel_id=1, replica_groups=mesh['slab_0'=8,'slab_1'=4,'slab_2'=2,'grp'=4] {'grp'}, dimensions={0}, use_global_device_ids=true | all-gather | bytes 737280 | tf_op jit(solution)/shard_map/all_gather | solution.py:51
  121.5 0.8 copy-done.1
  122.3 0.6 gather_fusion.2
  122.9 2.3 all-gather
  125.6 0.8 gather_fusion.3
  126.4 2.0 all-gather.3
  128.8 11.8 %all-gather.4 = f32[512,256]{1,0:T(8,128)S(1)} all-gather(f32[128,256]{1,0:T(8,128)S(1)} %convolution_add_fusion.29), channel_id=6, replica_groups=mesh['slab_0'=8,'slab_1'=4,'slab_2'=2,'grp'=4] {'slab_1'}, dimensions={0}, use_global_device_ids=true | all-gather | bytes 655360 | tf_op jit(solution)/shard_map/all_gather | solution.py:69
  140.6 9.4 %all-gather.1 = f32[512,128]{1,0:T(8,128)S(1)} all-gather(f32[128,128]{1,0:T(8,128)S(1)} %fusion.116), channel_id=3, replica_groups=mesh['slab_0'=8,'slab_1'=4,'slab_2'=2,'grp'=4] {'slab_1'}, dimensions={0}, use_global_device_ids=true | all-gather | bytes 327680 | tf_op jit(solution)/shard_map/all_gather | solution.py:69
  150.9 0.9 convolution_add_fusion.26
  152.3 0.6 slice-done.1
  153.0 0.6 gather_fusion.4
  153.6 6.6 %all-gather.6 = f32[256,128]{1,0:T(8,128)S(1)} all-gather(f32[128,128]{1,0:T(8,128)S(1)} %neg.28), channel_id=8, replica_groups=mesh['slab_0'=8,'slab_1'=4,'slab_2'=2,'grp'=4] {'slab_2'}, dimensions={0}, use_global_device_ids=true | all-gather | bytes 196608 | tf_op jit(solution)/shard_map/all_gather | solution.py:69
  160.6 10.4 %all-gather.7 = f32[512,128]{1,0:T(8,128)S(1)} all-gather(f32[128,128]{1,0:T(8,128)S(1)} %fusion.100), channel_id=9, replica_groups=mesh['slab_0'=8,'slab_1'=4,'slab_2'=2,'grp'=4] {'slab_1'}, dimensions={0}, use_global_device_ids=true | all-gather | bytes 327680 | tf_op jit(solution)/shard_map/all_gather | solution.py:69
  171.8 24.1 %all-gather.2 = f32[1024,128]{1,0:T(8,128)S(1)} all-gather(f32[128,128]{1,0:T(8,128)S(1)} %fusion.111), channel_id=4, replica_groups=mesh['slab_0'=8,'slab_1'=4,'slab_2'=2,'grp'=4] {'slab_0'}, dimensions={0}, use_global_device_ids=true | all-gather | bytes 589824 | tf_op jit(solution)/shard_map/all_gather | solution.py:69
  196.1 0.7 copy-done.4
  196.8 0.3 fusion.24
  197.4 1.2 convolution_add_fusion.32
  198.5 1.2 convolution_add_fusion.25
  199.7 1.2 convolution_add_fusion.24
  202.0 0.3 fusion
  202.8 8.6 %all-gather.9 = f32[256,256]{1,0:T(8,128)S(1)} all-gather(f32[128,256]{1,0:T(8,128)S(1)} %convolution_add_fusion.13), channel_id=11, replica_groups=mesh['slab_0'=8,'slab_1'=4,'slab_2'=2,'grp'=4] {'slab_2'}, dimensions={0}, use_global_device_ids=true | all-gather | bytes 393216 | tf_op jit(solution)/shard_map/all_gather | solution.py:69
  211.8 9.9 %all-gather.10 = f32[512,256]{1,0:T(8,128)S(1)} all-gather(f32[128,256]{1,0:T(8,128)S(1)} %convolution_add_fusion.12), channel_id=12, replica_groups=mesh['slab_0'=8,'slab_1'=4,'slab_2'=2,'grp'=4] {'slab_1'}, dimensions={0}, use_global_device_ids=true | all-gather | bytes 655360 | tf_op jit(solution)/shard_map/all_gather | solution.py:69
  221.9 0.3 convolution_add_fusion.11
  222.2 0.3 convolution_add_fusion.10
  222.5 0.9 convolution_add_fusion.9
  224.0 20.6 %all-gather.8 = f32[1024,128]{1,0:T(8,128)S(1)} all-gather(f32[128,128]{1,0:T(8,128)S(1)} %fusion.95), channel_id=10, replica_groups=mesh['slab_0'=8,'slab_1'=4,'slab_2'=2,'grp'=4] {'slab_0'}, dimensions={0}, use_global_device_ids=true | all-gather | bytes 589824 | tf_op jit(solution)/shard_map/all_gather | solution.py:69
  245.1 0.7 copy-done.5
  245.8 0.3 fusion.17
  246.3 11.4 %all-gather.17.cloned.1.call-done = f32[1024,256]{1,0:T(8,128)} async-done(((f32[128,256]{1,0:T(8,128)}), f32[1024,256]{1,0:T(8,128)}) %all-gather.17.cloned.1.call-update) | async-done | bytes 1048592 | tf_op jit(solution)/shard_map/all_gather | solution.py:69
  257.7 1.2 convolution_add_fusion.16
  258.9 1.2 convolution_add_fusion.8
  260.1 1.2 convolution_add_fusion.7
  261.8 0.3 convolution_add_fusion.4
  262.3 0.3 fusion.1
  263.2 12.8 %psum.60 = f32[256]{0:T(256)S(1)} all-reduce(f32[256]{0:T(256)S(1)} %get-tuple-element.8), channel_id=1, replica_groups=mesh['slab_0'=8,'slab_1'=4,'slab_2'=2,'grp'=4] {'slab_0'}, use_global_device_ids=true, to_apply=%region_6.7 | all-reduce | flops 256 | bytes 2048 | tf_op jit(solution)/shard_map/psum | solution.py:46
  276.0 8.3 %psum.61 = f32[256]{0:T(256)S(1)} all-reduce(f32[256]{0:T(256)S(1)} %psum.60), channel_id=1, replica_groups=mesh['slab_0'=8,'slab_1'=4,'slab_2'=2,'grp'=4] {'slab_1'}, use_global_device_ids=true, to_apply=%region_7.8 | all-reduce | flops 256 | bytes 2048 | tf_op jit(solution)/shard_map/psum | solution.py:46
  284.3 13.3 %psum.62 = f32[256]{0:T(256)S(1)} all-reduce(f32[256]{0:T(256)S(1)} %psum.61), channel_id=1, replica_groups=mesh['slab_0'=8,'slab_1'=4,'slab_2'=2,'grp'=4] {'slab_2'}, use_global_device_ids=true, to_apply=%region_8.9 | all-reduce | flops 256 | bytes 2048 | tf_op jit(solution)/shard_map/psum | solution.py:46
  297.6 8.4 %psum.63 = f32[256]{0:T(256)S(1)} all-reduce(f32[256]{0:T(256)S(1)} %psum.62), channel_id=1, replica_groups=mesh['slab_0'=8,'slab_1'=4,'slab_2'=2,'grp'=4] {'grp'}, use_global_device_ids=true, to_apply=%region_9.10 | all-reduce | flops 256 | bytes 2048 | tf_op jit(solution)/shard_map/psum | solution.py:46
  306.1 0.6 copy-done.18
  306.6 0.7 multiply_add_fusion
  (98 shorter events, 10.1 us)
Async XLA Ops:
  7.2 21.7 %copy-start = (f32[96,384]{1,0:T(8,128)S(1)}, f32[96,384]{1,0:T(8,128)}, u32[]{:S(2)}) copy-start(f32[96,384]{1,0:T(8,128)} %param.16) | copy-start | bytes 442372
  8.9 5.1 %copy-start.19 = (s32[1,128]{1,0:T(1,128)S(1)}, s32[1,128]{1,0:T(1,128)}, u32[]{:S(2)}) copy-start(s32[1,128]{1,0:T(1,128)} %param.19) | copy-start | bytes 1540
  8.9 11.4 %all-to-all-start = ((f32[4,96,256]{2,1,0:T(8,128)}), f32[4,96,256]{2,1,0:T(8,128)S(1)}, u32[]{:S(2)}, u32[]{:S(2)}) async-start(f32[4,96,256]{2,1,0:T(8,128)} %broadcast_in_dim.8), calls=%async_computation | async-start | bytes 786432 | tf_op jit(solution)/shard_map/all_to_all | solution.py:21
  21.0 8.3 %copy-start.12 = (f32[96,128]{1,0:T(8,128)S(1)}, f32[96,128]{1,0:T(8,128)}, u32[]{:S(2)}) copy-start(f32[96,128]{1,0:T(8,128)} %param.17) | copy-start | bytes 147460
  21.1 8.2 %collective-permute-start = (f32[1,128,256]{2,1,0:T(8,128)S(1)}, f32[1,128,256]{2,1,0:T(8,128)S(1)}, u32[]{:S(2)}, u32[]{:S(2)}) collective-permute-start(f32[1,128,256]{2,1,0:T(8,128)S(1)} %bitcast.105), channel_id=1, source_target_pairs={{0,4},{4,8},{8,12},{12,16},{16,20},{20,24},{24,28},{28,32},{32,36}... | collective-permute-start | bytes 393224 | tf_op jit(solution)/shard_map/ppermute | solution.py:36
  27.0 6.3 %collective-permute-start.1 = (f32[1,128,256]{2,1,0:T(8,128)S(1)}, f32[1,128,256]{2,1,0:T(8,128)S(1)}, u32[]{:S(2)}, u32[]{:S(2)}) collective-permute-start(f32[1,128,256]{2,1,0:T(8,128)S(1)} %bitcast.106), channel_id=1, source_target_pairs={{4,0},{8,4},{12,8},{16,12},{20,16},{24,20},{28,24},{32,28},{36,32}... | collective-permute-start | bytes 393224 | tf_op jit(solution)/shard_map/ppermute | solution.py:38
  29.3 4.0 %copy-start.8 = (f32[96,256]{1,0:T(8,128)S(1)}, f32[96,256]{1,0:T(8,128)}, u32[]{:S(2)}) copy-start(f32[96,256]{1,0:T(8,128)} %param.14) | copy-start | bytes 294916
  29.3 4.0 %copy-start.10 = (f32[96,128]{1,0:T(8,128)S(1)}, f32[96,128]{1,0:T(8,128)}, u32[]{:S(2)}) copy-start(f32[96,128]{1,0:T(8,128)} %param.18) | copy-start | bytes 147460
  29.6 42.3 %copy-start.13 = (f32[96,256]{1,0:T(8,128)S(1)}, f32[96,256]{1,0:T(8,128)}, u32[]{:S(2)}) copy-start(f32[96,256]{1,0:T(8,128)} %param.13) | copy-start | bytes 294916
  64.9 7.0 %copy-start.17 = (f32[256]{0:T(256)S(1)}, f32[256]{0:T(256)}, u32[]{:S(2)}) copy-start(f32[256]{0:T(256)} %param.15) | copy-start | bytes 3076
  71.9 0.8 copy-start.16
  72.7 190.2 %copy-start.3 = (f32[96,256]{1,0:T(8,128)}, f32[96,256]{1,0:T(8,128)S(1)}, u32[]{:S(2)}) copy-start(f32[96,256]{1,0:T(8,128)S(1)} %multiply_subtract_fusion) | copy-start | bytes 294916
  73.7 9.7 %all-to-all-start.1 = ((f32[4,96,256]{2,1,0:T(8,128)}), f32[4,96,256]{2,1,0:T(8,128)S(1)}, u32[]{:S(2)}, u32[]{:S(2)}) async-start(f32[4,96,256]{2,1,0:T(8,128)} %broadcast_in_dim.10), calls=%async_computation.1 | async-start | bytes 786432 | tf_op jit(solution)/shard_map/all_to_all | solution.py:21
  77.2 120.2 %all-gather.15.cloned.1.call-start = ((), (), s32[]{:S(2)}) async-start(), calls=%async_computation.2 | async-start | bytes 1179648 | tf_op jit(solution)/shard_map/all_gather | solution.py:69
  84.1 8.7 %collective-permute-start.2 = (f32[1,128,256]{2,1,0:T(8,128)S(1)}, f32[1,128,256]{2,1,0:T(8,128)S(1)}, u32[]{:S(2)}, u32[]{:S(2)}) collective-permute-start(f32[1,128,256]{2,1,0:T(8,128)S(1)} %bitcast.107), channel_id=1, source_target_pairs={{0,4},{4,8},{8,12},{12,16},{16,20},{20,24},{24,28},{28,32},{32,36}... | collective-permute-start | bytes 393224 | tf_op jit(solution)/shard_map/ppermute | solution.py:36
  90.5 6.3 %collective-permute-start.3 = (f32[1,128,256]{2,1,0:T(8,128)S(1)}, f32[1,128,256]{2,1,0:T(8,128)S(1)}, u32[]{:S(2)}, u32[]{:S(2)}) collective-permute-start(f32[1,128,256]{2,1,0:T(8,128)S(1)} %bitcast.108), channel_id=1, source_target_pairs={{4,0},{8,4},{12,8},{16,12},{20,16},{24,20},{28,24},{32,28},{36,32}... | collective-permute-start | bytes 393224 | tf_op jit(solution)/shard_map/ppermute | solution.py:38
  93.1 4.0 %copy-start.11 = (f32[96,128]{1,0:T(8,128)S(1)}, f32[96,128]{1,0:T(8,128)}, u32[]{:S(2)}) copy-start(f32[96,128]{1,0:T(8,128)} %param.23) | copy-start | bytes 147460
  93.1 4.0 %copy-start.15 = (f32[96,128]{1,0:T(8,128)S(1)}, f32[96,128]{1,0:T(8,128)}, u32[]{:S(2)}) copy-start(f32[96,128]{1,0:T(8,128)} %param.22) | copy-start | bytes 147460
  97.1 11.6 %copy-start.9 = (f32[96,384]{1,0:T(8,128)S(1)}, f32[96,384]{1,0:T(8,128)}, u32[]{:S(2)}) copy-start(f32[96,384]{1,0:T(8,128)} %param.21) | copy-start | bytes 442372
  108.7 12.7 %copy-start.2 = (f32[384,512]{1,0:T(8,128)}, f32[384,512]{1,0:T(8,128)S(1)}, u32[]{:S(2)}) copy-start(f32[384,512]{1,0:T(8,128)S(1)} %all_gather.74) | copy-start | bytes 2359300
  121.5 0.8 copy-start.1
  122.9 2.7 slice-start
  152.1 0.9 slice-start.1
  152.3 105.4 %all-gather.17.cloned.1.call-start = ((), (), s32[]{:S(2)}) async-start(), calls=%async_computation.3 | async-start | bytes 1179648 | tf_op jit(solution)/shard_map/all_gather | solution.py:69
  195.9 0.9 copy-start.4
  197.3 3.5 %copy-start.6 = (f32[1024,256]{1,0:T(8,128)S(1)}, f32[1024,256]{1,0:T(8,128)}, u32[]{:S(2)}) copy-start(f32[1024,256]{1,0:T(8,128)} %all-gather.15.cloned.1.call-done) | copy-start | bytes 3145732
  244.9 0.9 copy-start.5
  257.7 3.5 %copy-start.7 = (f32[1024,256]{1,0:T(8,128)S(1)}, f32[1024,256]{1,0:T(8,128)}, u32[]{:S(2)}) copy-start(f32[1024,256]{1,0:T(8,128)} %all-gather.17.cloned.1.call-done) | copy-start | bytes 3145732
  262.9 43.7 %copy-start.14 = (f32[96,256]{1,0:T(8,128)S(1)}, f32[96,256]{1,0:T(8,128)}, u32[]{:S(2)}) copy-start(f32[96,256]{1,0:T(8,128)} %param.12) | copy-start | bytes 294916
  306.0 0.6 copy-start.18
Sparse Core Ops, SparseCore 0:
  152.4 38.5 all-gather.14
  223.5 34.1 all-gather.16
where the time goes:
time: 315 us; the launch traced here: 314 us
  blocking collectives  210 us (67%)
  waiting for transfers between devices  31.1 us (10%)
  starting transfers between devices  24.8 us (8%)
  matrix products  21.9 us (7%)
  between operations  14.9 us (5%)
  local copies, waits for them, and re-layouts  10.2 us (3%)
    all_gather x10, blocking collectives, entering(): pieces = jax.tree.map(lambda part: lax.all_gather(part, axis), subtotal)  106 us
    psum x8, blocking collectives, by_axis(): return functools.reduce(lax.psum, axes, x)  81.2 us
    all_gather x2, blocking collectives, sent_together(): result, at, done = (lax.all_gather(both, axis, axis=dim, tiled=True), 0, [])  23.6 us
    dot_general x62, matrix products, matmul(): jnp.dot(left, right, precision=lax.Precision.HIGHEST, preferred_element_t...  21.9 us
    all_to_all x2, waiting for transfers between devices, sent_to_all(): return lax.all_to_all(copies, axis, split_axis=0, concat_axis=0, tiled=True)  12.3 us
    ppermute x2, starting transfers between devices, extended(): lax.ppermute(tail, axis, [(i, (i + 1) % count) for i in range(ends)])  12.3 us
    all_gather x2, waiting for transfers between devices, entering(): pieces = jax.tree.map(lambda part: lax.all_gather(part, axis), subtotal)  11.4 us
    all_to_all x2, starting transfers between devices, sent_to_all(): return lax.all_to_all(copies, axis, split_axis=0, concat_axis=0, tiled=True)  8.59 us
  transfers between devices with their start and end apart: 8, of which 5 were waited for; matrix products, arithmetic and copies ran while one was open for 2% of the time, Pallas kernels for 0%

commit v1 on v0

v1 whole, which is shorter than its diff:
```python
import functools

import jax
import jax.numpy as jnp
from jax import lax
from jax.experimental import pallas as pl
from jax.experimental.pallas import tpu as pltpu
from jax.sharding import Mesh
from jax.sharding import PartitionSpec as P

SLAB = ("slab_0", "slab_1", "slab_2")
PLANE = ("slab_1", "slab_2")
SLAB_GRP = ("slab_0", "slab_1", "slab_2", "grp")
HIGH = lax.Precision.HIGHEST


def mm(left, right, left_dim=1, right_dim=0):
    return lax.dot_general(
        left,
        right,
        (((left_dim,), (right_dim,)), ((), ())),
        precision=HIGH,
        preferred_element_type=jnp.float32,
    )


def to_each(pieces, axes):
    return lax.all_to_all(pieces, axes, split_axis=0, concat_axis=0, tiled=True)


def to_all(x, axes, count):
    return to_each(jnp.broadcast_to(x, (count, *x.shape)), axes)


def beside(faces):
    count = lax.axis_size(SLAB)
    below = lax.ppermute(faces, SLAB, [(i, i + 1) for i in range(count - 1)])
    above = lax.ppermute(faces, SLAB, [(i + 1, i) for i in range(count - 1)])
    return below, above


def swapped(rows):
    half = rows.shape[0] // 2
    return jnp.concatenate([rows[half:], rows[:half]], axis=0)


def in_lanes(first, second, shape):
    lane = lax.broadcasted_iota(jnp.int32, shape, 1)
    return jnp.where(lane == 0, first, jnp.where(lane == 1, second, 0.0))


def sweep_plane(got_ref, states_f_ref, states_b_ref, maps_ref, sums_ref):
    n = got_ref.shape[0]
    width = got_ref.shape[2]
    row = lax.broadcasted_iota(jnp.int32, (width, width), 0)
    lane = lax.broadcasted_iota(jnp.int32, (width, width), 1)
    eye = jnp.where(row == lane, 1.0, 0.0).astype(jnp.float32)
    f = jnp.concatenate([eye, jnp.zeros((16, width), jnp.float32)], axis=0)
    empty = jnp.zeros((width, width), jnp.float32)
    passed = []
    for i in range(n):
        states_f_ref[i] = f
        f = mm(f, got_ref[i, 0:128], 1, 1)
        f = jnp.concatenate([f[:128], f[128:] + got_ref[i, 256:272]], axis=0)
        passed.append(f)
    b = jnp.concatenate([eye, empty, jnp.zeros((16, width), jnp.float32)], axis=0)
    for i in reversed(range(n)):
        states_b_ref[i] = b
        b = mm(b, got_ref[i, 128:256], 1, 1)
        b = jnp.concatenate([b[:128], b[128:] + passed[i]], axis=0)
    maps_ref[0] = f[:128]
    maps_ref[1] = b[:128]
    maps_ref[2] = b[128:256]
    gamma = jnp.zeros((16, width), jnp.float32)
    delta = gamma
    same = gamma
    cross = gamma
    total = jnp.zeros((8, width), jnp.float32)
    for i in range(n):
        g = got_ref[i, 272:288]
        h = got_ref[i, 288:304]
        total = total + got_ref[i, 304:312]
        gamma = gamma + mm(g, states_f_ref[i, 0:128], 1, 1) + mm(h, states_b_ref[i, 128:256], 1, 1)
        delta = delta + mm(h, states_b_ref[i, 0:128], 1, 1)
        own_f = states_f_ref[i, 128:144]
        own_b = states_b_ref[i, 256:272]
        same = same + g * own_f + h * own_b
        cross = cross + g * swapped(own_f) + h * swapped(own_b)
    sums_ref[0:16] = f[128:]
    sums_ref[16:32] = b[256:]
    sums_ref[32:48] = gamma
    sums_ref[48:64] = delta
    sums_ref[64:80] = in_lanes(
        jnp.sum(same, axis=1, keepdims=True), jnp.sum(cross, axis=1, keepdims=True), (16, width)
    )
    sums_ref[80:88] = total


def solve_planes(place_ref, sums_ref, maps_ref, states_f_ref, states_b_ref, out_ref, total_ref, f_ref, b_ref):
    n = sums_ref.shape[0]
    width = sums_ref.shape[2]

    def whole(z, which):
        return jnp.concatenate(
            [maps_ref[p, z, 16 * which : 16 * which + 16] for p in range(maps_ref.shape[0])], axis=0
        )

    f = jnp.zeros((16, width), jnp.float32)
    for z in range(n):
        f_ref[z] = f
        if z + 1 < n:
            f = mm(f, whole(z, 0)) + sums_ref[z, 0:16]
    b = jnp.zeros((16, width), jnp.float32)
    for z in reversed(range(n)):
        b_ref[z] = b
        if z > 0:
            b = mm(b, whole(z, 1)) + (mm(f_ref[z], whole(z, 2)) + sums_ref[z, 16:32])
    same = jnp.zeros((16, width), jnp.float32)
    cross = same
    known = same
    total = jnp.zeros((8, width), jnp.float32)
    for z in range(n):
        gamma = sums_ref[z, 32:48]
        delta = sums_ref[z, 48:64]
        f = f_ref[z]
        b = b_ref[z]
        same = same + gamma * f + delta * b
        cross = cross + gamma * swapped(f) + delta * swapped(b)
        known = known + sums_ref[z, 64:80]
        total = total + sums_ref[z, 80:88]
    dots = known + in_lanes(
        jnp.sum(same, axis=1, keepdims=True), jnp.sum(cross, axis=1, keepdims=True), (16, width)
    )
    total_ref[...] = total
    f = f_ref[place_ref[0]]
    b = b_ref[place_ref[0]]
    for i in range(states_f_ref.shape[0]):
        out_ref[i, 0:16] = mm(f, states_f_ref[i, 0:128]) + states_f_ref[i, 128:144]
        out_ref[i, 16:32] = (
            mm(b, states_b_ref[i, 0:128]) + mm(f, states_b_ref[i, 128:256]) + states_b_ref[i, 256:272]
        )
        out_ref[i, 32:48] = dots


def shaped(*shape):
    return jax.ShapeDtypeStruct(shape, jnp.float32)


VMEM = pl.BlockSpec(memory_space=pltpu.VMEM)
SMEM = pl.BlockSpec(memory_space=pltpu.SMEM)


def plane_kernel(got):
    n, _, width = got.shape
    return pl.pallas_call(
        sweep_plane,
        out_shape=(
            shaped(n, 144, width),
            shaped(n, 272, width),
            shaped(3, 128, width),
            shaped(88, width),
        ),
        in_specs=[VMEM],
        out_specs=(VMEM, VMEM, VMEM, VMEM),
        name="sweep_plane",
    )(got)


def planes_kernel(place, sums, maps, states_f, states_b):
    n = sums.shape[0]
    width = sums.shape[2]
    return pl.pallas_call(
        solve_planes,
        out_shape=(shaped(states_f.shape[0], 48, width), shaped(8, width)),
        in_specs=[SMEM, VMEM, VMEM, VMEM, VMEM],
        out_specs=(VMEM, VMEM),
        scratch_shapes=[pltpu.VMEM((n, 16, width), jnp.float32), pltpu.VMEM((n, 16, width), jnp.float32)],
        name="solve_planes",
    )(place, sums, maps, states_f, states_b)


def sliced(rows):
    two, n, each = 2, 8, rows.shape[0] // 16
    return rows.reshape(two, n, each, -1).transpose(1, 0, 2, 3).reshape(n, two * each, -1)


def joined(pieces):
    n, both, width = pieces.shape
    return pieces.reshape(n, 2, both // 2, width).transpose(1, 0, 2, 3).reshape(n * both, width)


def local(
    iterate,
    residual,
    direction,
    prior_rho,
    diag_blocks,
    lower_coupling,
    upper_coupling,
    interface,
    jacobi_inverse,
    slab_inverse,
    lower_factor,
    upper_factor,
):
    index_rows = interface[0]
    rows, cols = direction.shape
    groups = lax.axis_size("grp")
    part = cols // groups
    fields = to_each(
        jnp.stack(
            [
                jnp.concatenate(
                    [direction[:, q * part : (q + 1) * part], residual[:, q * part : (q + 1) * part]], axis=1
                )
                for q in range(groups)
            ]
        ),
        "grp",
    ).reshape(groups * rows, 2 * part)
    d = fields[:, :part]
    operator = to_all(
        jnp.concatenate([diag_blocks, lower_coupling, upper_coupling], axis=1), "grp", groups
    ).reshape(groups * rows, -1)
    coarse = to_all(
        jnp.concatenate([slab_inverse, lower_factor, upper_factor, jacobi_inverse], axis=1), "grp", groups
    )
    jacobi = coarse[:, :, 640:]
    coarse = coarse.reshape(groups * rows, -1)
    inverse = coarse[:, 0:384]
    lower = coarse[:, 384:512]
    upper = coarse[:, 512:640]

    below, above = beside(d[index_rows])
    w = mm(operator, jnp.concatenate([d, below, above], axis=0))
    x = jnp.concatenate([fields[:, part:], w], axis=1)
    smoothed = lax.dot_general(
        jacobi,
        x.reshape(groups, rows, 2 * part),
        (((2,), (1,)), ((0,), (0,))),
        precision=HIGH,
        preferred_element_type=jnp.float32,
    ).reshape(groups * rows, 2 * part)
    below, above = beside(smoothed[index_rows])
    defect = x - mm(operator, jnp.concatenate([smoothed, below, above], axis=0))
    both = mm(inverse, jnp.concatenate([defect, lower], axis=1))
    solved, factor = both[:, :128], both[:, 128:]
    at_faces = jnp.concatenate([both, upper], axis=1)[index_rows]
    maps = -at_faces[:, 128:]
    pulled = -mm(x, jnp.concatenate([factor, upper], axis=1), 0, 0)
    y = smoothed + solved
    y_swapped = jnp.concatenate([y[:, part:], y[:, :part]], axis=1)
    d_w = jnp.sum(d * w, axis=0)
    known = jnp.stack(
        [jnp.sum(x * y, axis=0), jnp.sum(x * y_swapped, axis=0), jnp.concatenate([d_w, d_w])]
        + [jnp.zeros((2 * part,), jnp.float32)] * 5
    )
    n_plane = lax.axis_size(PLANE)
    n_z = lax.axis_size("slab_0")
    got = to_each(
        jnp.concatenate(
            [
                jnp.broadcast_to(jnp.concatenate([maps[:, :128], maps[:, 128:]], axis=0), (n_plane, 256, 128)),
                sliced(at_faces[:, :128].T),
                sliced(pulled[:, :128]),
                sliced(pulled[:, 128:]),
                jnp.broadcast_to(known, (n_plane, 8, 128)),
            ],
            axis=1,
        ),
        PLANE,
    )
    states_f, states_b, plane_maps, plane_sums = plane_kernel(got)
    own = lax.dynamic_slice_in_dim(plane_maps, 16 * lax.axis_index(PLANE), 16, axis=1).reshape(48, 128)
    sums = to_all(jnp.concatenate([plane_sums, own], axis=0), "slab_0", n_z)
    all_maps = to_all(sums[:, 88:], PLANE, n_plane)
    place = lax.axis_index("slab_0").astype(jnp.int32).reshape(1)
    entering, total = planes_kernel(place, sums, all_maps, states_f, states_b)
    back = to_each(entering, PLANE)
    f = joined(back[:, 0:16])
    b = joined(back[:, 16:32])
    dots = joined(back[:, 32:48]).T
    own_part = lax.dynamic_slice_in_dim(prior_rho, part * lax.axis_index("grp"), part)
    step_size = own_part / total[2, :part]
    same = total[0] + dots[0]
    cross = total[1] + dots[1]
    new_rho = (
        same[:part] - step_size * (cross[:part] + cross[part:]) + step_size * (step_size * same[part:])
    )
    precond = smoothed + mm(inverse, defect - mm(lower, f, 1, 1)) - mm(upper, b, 1, 1)
    result = precond[:, :part] - step_size * precond[:, part:]
    scales = jnp.broadcast_to(jnp.concatenate([step_size, new_rho]), (groups, 8, 2 * part))
    sent = jnp.concatenate(
        [jnp.concatenate([result, w], axis=1).reshape(groups, rows, 2 * part), scales], axis=1
    )
    out = to_each(sent, "grp")
    result = jnp.concatenate([out[q, :rows, :part] for q in range(groups)], axis=1)
    image = jnp.concatenate([out[q, :rows, part:] for q in range(groups)], axis=1)
    step_size = jnp.concatenate([out[q, rows, :part] for q in range(groups)])
    new_rho = jnp.concatenate([out[q, rows, part:] for q in range(groups)])
    new_iterate = iterate + step_size * direction
    new_residual = residual - step_size * image
    new_direction = result + new_rho / prior_rho * direction
    return (new_iterate, new_residual, new_direction, new_rho)


def solution(mesh):
    split = Mesh(
        mesh.devices.reshape(8, 4, 2, mesh.shape["grp"]), ("slab_0", "slab_1", "slab_2", "grp")
    )
    rows = P(SLAB_GRP, None)
    placed = (rows, rows, rows, P(), rows, rows, rows, P(SLAB, None), rows, rows, rows, rows)
    return jax.shard_map(
        local, mesh=split, in_specs=placed, out_specs=(rows, rows, rows, P()), check_vma=False
    )
```

time: 315 us -> 192 us (0.61)
  blocking collectives: 210 us -> 32 us
  waiting for transfers between devices: 31.1 us -> 66.3 us
  starting transfers between devices: 24.8 us -> 46.8 us
  Pallas kernels: 0 us -> 16.5 us
  matrix products: 21.9 us -> 5.6 us
  between operations: 14.9 us -> 1.2 us
  local copies, waits for them, and re-layouts: 10.2 us -> 16.9 us
  other arithmetic: 0.77 us -> 5.28 us
    all_gather x12 -> x0, blocking collectives: 129 us -> none  [the longest x10 106 us: entering(): pieces = jax.tree.map(lambda part: lax.all_gather(part, axis), subtotal)]
    psum x8 -> x0, blocking collectives: 81.2 us -> none  [by_axis(): return functools.reduce(lax.psum, axes, x)]
    all_to_all x2 -> x6, waiting for transfers between devices: 12.3 us -> 60.4 us  [to_each(): return lax.all_to_all(pieces, axes, split_axis=0, concat_axis=0, tiled=True)]
    all_to_all x0 -> x2, blocking collectives: none -> 32 us  [to_each(): return lax.all_to_all(pieces, axes, split_axis=0, concat_axis=0, tiled=True)]
    all_to_all x2 -> x6, starting transfers between devices: 8.59 us -> 29.5 us  [to_each(): return lax.all_to_all(pieces, axes, split_axis=0, concat_axis=0, tiled=True)]
    pallas_call x0 -> x2, Pallas kernels: none -> 16.5 us  [the longest x1 9.61 us: plane_kernel(): pl.pallas_call(sweep_plane, out_shape=(shaped(n, 144, width), shaped(n, 2...]
    dot_general x62 -> x8, matrix products: 21.9 us -> 5.6 us  [the longest x7 5.27 us: mm(): lax.dot_general(left, right, (((left_dim,), (right_dim,)), ((), ())), pre...]
    all_gather x2 -> x0, waiting for transfers between devices: 11.4 us -> none  [entering(): pieces = jax.tree.map(lambda part: lax.all_gather(part, axis), subtotal)]
  transfers between devices with their start and end apart: 8 -> 10, of which waited for: 5 -> 7; matrix products, arithmetic and copies ran while one was open for 2% -> 2% of each run, Pallas kernels for 0% -> 0%
where the time goes in v1:
time: 192 us; the launch traced here: 191 us
  waiting for transfers between devices  66.3 us (35%)
  starting transfers between devices  46.8 us (24%)
  blocking collectives  32 us (17%)
  local copies, waits for them, and re-layouts  16.9 us (9%)
  Pallas kernels  16.5 us (9%)
  matrix products  5.6 us (3%)
  other arithmetic  5.28 us (3%)
    all_to_all x6, waiting for transfers between devices, to_each(): return lax.all_to_all(pieces, axes, split_axis=0, concat_axis=0, tiled=True)  60.4 us
    all_to_all x2, blocking collectives, to_each(): return lax.all_to_all(pieces, axes, split_axis=0, concat_axis=0, tiled=True)  32 us
    all_to_all x6, starting transfers between devices, to_each(): return lax.all_to_all(pieces, axes, split_axis=0, concat_axis=0, tiled=True)  29.5 us
    ppermute x2, starting transfers between devices, beside(): below = lax.ppermute(faces, SLAB, [(i, i + 1) for i in range(count - 1)])  13.4 us
    pallas_call x1, Pallas kernels, plane_kernel(): pl.pallas_call(sweep_plane, out_shape=(shaped(n, 144, width), shaped(n, 2...  9.61 us
    pallas_call x1, Pallas kernels, planes_kernel(): pl.pallas_call(solve_planes, out_shape=(shaped(states_f.shape[0], 48, wid...  6.93 us
    unnamed x47, local copies, waits for them, and re-layouts  5.96 us
    ppermute x2, waiting for transfers between devices, beside(): above = lax.ppermute(faces, SLAB, [(i + 1, i) for i in range(count - 1)])  5.88 us
  transfers between devices with their start and end apart: 10, of which 7 were waited for; matrix products, arithmetic and copies ran while one was open for 2% of the time, Pallas kernels for 0%

profile of v1, /device:TPU:1, one launch (start us, length us, event | category | flops | bytes accessed | tf_op | source)
XLA Modules:
  0.0 190.6 jit_solution(3032602601973986937)
XLA Ops:
  0.7 1.0 fusion.40
  1.7 1.0 fusion.41
  2.6 0.1 maximum_bitcast_fusion
  2.8 0.7 pad_maximum_fusion.6
  3.5 5.0 %all-to-all-start.1 = ((f32[4,96,128]{2,1,0:T(8,128)}), f32[4,96,128]{2,1,0:T(8,128)S(1)}, u32[]{:S(2)}, u32[]{:S(2)}) async-start(f32[4,96,128]{2,1,0:T(8,128)} %pad_maximum_fusion.6), calls=%async_computation.1 | async-start | bytes 393216 | tf_op jit(solution)/shard_map/all_to_all | solution.py:28
  8.6 5.1 %all-to-all-done.1 = f32[4,96,128]{2,1,0:T(8,128)S(1)} async-done(((f32[4,96,128]{2,1,0:T(8,128)}), f32[4,96,128]{2,1,0:T(8,128)S(1)}, u32[]{:S(2)}, u32[]{:S(2)}) %all-to-all-start.1) | async-done | bytes 196640 | tf_op jit(solution)/shard_map/all_to_all | solution.py:28
  13.7 1.0 broadcast_in_dim.29
  14.8 3.7 %all-to-all-start.2 = ((f32[4,96,640]{2,1,0:T(8,128)}), f32[4,96,640]{2,1,0:T(8,128)S(1)}, u32[]{:S(2)}, u32[]{:S(2)}) async-start(f32[4,96,640]{2,1,0:T(8,128)} %broadcast_in_dim.29), calls=%async_computation.2 | async-start | bytes 1966080 | tf_op jit(solution)/shard_map/all_to_all | solution.py:28
  18.5 11.4 %all-to-all-done.2 = f32[4,96,640]{2,1,0:T(8,128)S(1)} async-done(((f32[4,96,640]{2,1,0:T(8,128)}), f32[4,96,640]{2,1,0:T(8,128)S(1)}, u32[]{:S(2)}, u32[]{:S(2)}) %all-to-all-start.2) | async-done | bytes 983072 | tf_op jit(solution)/shard_map/all_to_all | solution.py:28
  29.9 1.1 broadcast_in_dim.28
  31.0 3.5 %all-to-all-start = ((f32[4,96,736]{2,1,0:T(8,128)}), f32[4,96,736]{2,1,0:T(8,128)S(1)}, u32[]{:S(2)}, u32[]{:S(2)}) async-start(f32[4,96,736]{2,1,0:T(8,128)} %broadcast_in_dim.28), calls=%async_computation | async-start | bytes 2359296 | tf_op jit(solution)/shard_map/all_to_all | solution.py:28
  34.6 0.1 fusion.37
  34.7 0.7 gather_fusion
  35.4 6.9 %collective-permute-start = (f32[128,64]{0,1:T(8,128)S(1)}, f32[128,64]{0,1:T(8,128)S(1)}, u32[]{:S(2)}, u32[]{:S(2)}) collective-permute-start(f32[128,64]{0,1:T(8,128)S(1)} %copy.35), channel_id=1, source_target_pairs={{0,4},{4,8},{8,12},{12,16},{16,20},{20,24},{24,28},{28,32},{32,36}... | collective-permute-start | bytes 98312 | tf_op jit(solution)/shard_map/ppermute | solution.py:37
  42.3 1.9 %collective-permute-start.1 = (f32[128,64]{0,1:T(8,128)S(1)}, f32[128,64]{0,1:T(8,128)S(1)}, u32[]{:S(2)}, u32[]{:S(2)}) collective-permute-start(f32[128,64]{0,1:T(8,128)S(1)} %copy.35), channel_id=1, source_target_pairs={{4,0},{8,4},{12,8},{16,12},{20,16},{24,20},{28,24},{32,28},{36,32}... | collective-permute-start | bytes 98312 | tf_op jit(solution)/shard_map/ppermute | solution.py:38
  44.2 0.1 copy.53
  44.3 0.1 copy.52
  44.5 3.4 %collective-permute-done.1 = f32[128,64]{0,1:T(8,128)S(1)} collective-permute-done((f32[128,64]{0,1:T(8,128)S(1)}, f32[128,64]{0,1:T(8,128)S(1)}, u32[]{:S(2)}, u32[]{:S(2)}) %collective-permute-start.1) | collective-permute-done | bytes 32800 | tf_op jit(solution)/shard_map/ppermute | solution.py:38
  47.8 1.2 multiply_reduce_fusion.1
  49.1 0.1 copy.37
  49.3 0.3 fusion.14
  49.6 0.6 gather_fusion.1
  50.3 6.6 %collective-permute-start.2 = (f32[128,128]{1,0:T(8,128)S(1)}, f32[128,128]{1,0:T(8,128)S(1)}, u32[]{:S(2)}, u32[]{:S(2)}) collective-permute-start(f32[128,128]{1,0:T(8,128)S(1)} %gather_fusion.1), channel_id=1, source_target_pairs={{0,4},{4,8},{8,12},{12,16},{16,20},{20,24},{24,28},{28,32},{32,36}... | collective-permute-start | bytes 196616 | tf_op jit(solution)/shard_map/ppermute | solution.py:37
  56.9 1.9 %collective-permute-start.3 = (f32[128,128]{1,0:T(8,128)S(1)}, f32[128,128]{1,0:T(8,128)S(1)}, u32[]{:S(2)}, u32[]{:S(2)}) collective-permute-start(f32[128,128]{1,0:T(8,128)S(1)} %gather_fusion.1), channel_id=1, source_target_pairs={{4,0},{8,4},{12,8},{16,12},{20,16},{24,20},{28,24},{32,28},{36,32}... | collective-permute-start | bytes 196616 | tf_op jit(solution)/shard_map/ppermute | solution.py:38
  58.8 0.8 copy.47
  59.7 0.1 copy.54
  59.8 0.1 copy.55
  59.9 2.5 %collective-permute-done.3 = f32[128,128]{1,0:T(8,128)S(1)} collective-permute-done((f32[128,128]{1,0:T(8,128)S(1)}, f32[128,128]{1,0:T(8,128)S(1)}, u32[]{:S(2)}, u32[]{:S(2)}) %collective-permute-start.3) | collective-permute-done | bytes 65568 | tf_op jit(solution)/shard_map/ppermute | solution.py:38
  62.4 1.1 convolution_subtract_fusion.2
  63.6 0.9 fusion.1
  64.6 0.2 copy.40
  64.8 0.8 gather_fusion.2
  65.6 0.1 copy-done.3
  65.8 0.5 convolution_negate_fusion
  66.3 1.0 broadcast_dynamic-update-slice_fusion
  67.5 0.1 fusion.16
  67.6 0.7 bitcast_dynamic-update-slice_fusion.2
  68.3 0.6 bitcast_dynamic-update-slice_fusion.1
  68.9 0.6 bitcast_dynamic-update-slice_fusion
  69.6 0.6 broadcast_dynamic-update-slice_fusion.1
  70.2 6.6 %all-to-all-start.3 = ((f32[8,312,128]{2,1,0:T(8,128)}), f32[8,312,128]{2,1,0:T(8,128)S(1)}, u32[]{:S(2)}, u32[]{:S(2)}) async-start(f32[8,312,128]{2,1,0:T(8,128)} %broadcast_dynamic-update-slice_fusion.1), calls=%async_computation.3 | async-start | bytes 2555904 | tf_op jit(solution)/shard_map/all_to_all | solution.py:28
  76.8 17.4 %all-to-all-done.3.got_ref = f32[8,312,128]{2,1,0:T(8,128)S(1)} async-done(((f32[8,312,128]{2,1,0:T(8,128)}), f32[8,312,128]{2,1,0:T(8,128)S(1)}, u32[]{:S(2)}, u32[]{:S(2)}) %all-to-all-start.3) | async-done | bytes 1277984 | tf_op jit(solution)/shard_map/all_to_all | solution.py:28
  94.2 1.1 copy-done.1
  95.3 9.6 %sweep_plane.1 = (f32[8,144,128]{2,1,0:T(8,128)}, f32[8,272,128]{2,1,0:T(8,128)}, f32[3,128,128]{2,1,0:T(8,128)}, f32[88,128]{1,0:T(8,128)}) custom-call(f32[8,312,128]{2,1,0:T(8,128)} %copy-done.1), custom_call_target="tpu_custom_call" | custom-call | tf_op jit(solution)/shard_map/sweep_plane/pallas_call | solution.py:155
  104.9 0.7 constant_dynamic-slice_fusion
  105.7 0.8 pad_maximum_fusion.8
  106.5 24.1 %all_to_all.40.sums_ref = f32[8,136,128]{2,1,0:T(8,128)S(1)} all-to-all(f32[8,136,128]{2,1,0:T(8,128)S(1)} %broadcast_in_dim.32), channel_id=1, replica_groups=mesh['slab_0'=8,'slab_1'=4,'slab_2'=2,'grp'=4] {'slab_0'}, dimensions={0} | all-to-all | bytes 1114112 | tf_op jit(solution)/shard_map/all_to_all | solution.py:28
  130.6 1.3 broadcast_in_dim.33
  131.9 6.4 %all-to-all-start.5 = ((f32[8,8,48,128]{3,2,1,0:T(8,128)}), f32[8,8,48,128]{3,2,1,0:T(8,128)S(1)}, u32[]{:S(2)}, u32[]{:S(2)}) async-start(f32[8,8,48,128]{3,2,1,0:T(8,128)} %broadcast_in_dim.33), calls=%async_computation.5 | async-start | bytes 3145728 | tf_op jit(solution)/shard_map/all_to_all | solution.py:28
  138.3 20.6 %all-to-all-done.5.maps_ref = f32[8,8,48,128]{3,2,1,0:T(8,128)S(1)} async-done(((f32[8,8,48,128]{3,2,1,0:T(8,128)}), f32[8,8,48,128]{3,2,1,0:T(8,128)S(1)}, u32[]{:S(2)}, u32[]{:S(2)}) %all-to-all-start.5) | async-done | bytes 1572896 | tf_op jit(solution)/shard_map/all_to_all | solution.py:28
  158.9 1.2 copy-done
  160.1 6.9 %solve_planes.1 = (f32[8,48,128]{2,1,0:T(8,128)}, f32[8,128]{1,0:T(8,128)}) custom-call(s32[1]{0:T(128)} %bitcast.11.place_ref, f32[8,136,128]{2,1,0:T(8,128)} %copy-done.2, f32[8,8,48,128]{3,2,1,0:T(8,128)} %copy-done, f32[8,144,128]{2,1,0:T(8,128)} %get-tuple-element.12.states_f_ref, f32[8,272,128]{2,1,0:T(8,128)} %get-tuple-element.13.states_b_ref), custom_call_target="tpu_custom_call" | custom-call | tf_op jit(solution)/shard_map/solve_planes/pallas_call | solution.py:172
  167.0 4.4 %all-to-all-start.6 = ((f32[8,48,128]{2,1,0:T(8,128)}), f32[8,48,128]{2,1,0:T(8,128)S(1)}, u32[]{:S(2)}, u32[]{:S(2)}) async-start(f32[8,48,128]{2,1,0:T(8,128)} %get-tuple-element.14), calls=%async_computation.6 | async-start | bytes 393216 | tf_op jit(solution)/shard_map/all_to_all | solution.py:28
  171.4 5.9 %all-to-all-done.6 = f32[8,48,128]{2,1,0:T(8,128)S(1)} async-done(((f32[8,48,128]{2,1,0:T(8,128)}), f32[8,48,128]{2,1,0:T(8,128)S(1)}, u32[]{:S(2)}, u32[]{:S(2)}) %all-to-all-start.6) | async-done | bytes 196640 | tf_op jit(solution)/shard_map/all_to_all | solution.py:28
  177.4 0.4 convolution_subtract_fusion.1
  177.8 0.7 convolution_add_fusion
  178.6 0.4 convolution_subtract_fusion
  179.0 0.8 slice_add_fusion.1
  179.8 0.8 fusion.25
  180.7 0.1 copy.49
  181.0 7.9 %all_to_all.41 = f32[4,104,128]{2,1,0:T(8,128)S(1)} all-to-all(f32[4,104,128]{2,1,0:T(8,128)S(1)} %pad_maximum_fusion.5), channel_id=1, replica_groups=mesh['slab_0'=8,'slab_1'=4,'slab_2'=2,'grp'=4] {'grp'}, dimensions={0} | all-to-all | bytes 425984 | tf_op jit(solution)/shard_map/all_to_all | solution.py:28
  189.0 0.6 fusion.34
  189.6 0.1 slice_bitcast_fusion.7
  189.8 0.8 maximum_add_fusion
  (73 shorter events, 1.2 us)
Async XLA Ops:
  0.6 7.9 %copy-start.9 = (f32[96,384]{1,0:T(8,128)S(1)}, f32[96,384]{1,0:T(8,128)}, u32[]{:S(2)}) copy-start(f32[96,384]{1,0:T(8,128)} %param.16) | copy-start | bytes 442372
  0.6 7.9 %copy-start.16 = (f32[96,128]{1,0:T(8,128)S(1)}, f32[96,128]{1,0:T(8,128)}, u32[]{:S(2)}) copy-start(f32[96,128]{1,0:T(8,128)} %param.17) | copy-start | bytes 147460
  0.7 7.9 %copy-start.15 = (f32[96,128]{1,0:T(8,128)S(1)}, f32[96,128]{1,0:T(8,128)}, u32[]{:S(2)}) copy-start(f32[96,128]{1,0:T(8,128)} %param.18) | copy-start | bytes 147460
  3.5 10.2 %all-to-all-start.1 = ((f32[4,96,128]{2,1,0:T(8,128)}), f32[4,96,128]{2,1,0:T(8,128)S(1)}, u32[]{:S(2)}, u32[]{:S(2)}) async-start(f32[4,96,128]{2,1,0:T(8,128)} %pad_maximum_fusion.6), calls=%async_computation.1 | async-start | bytes 393216 | tf_op jit(solution)/shard_map/all_to_all | solution.py:28
  14.8 3.7 %copy-start.10 = (f32[96,384]{1,0:T(8,128)S(1)}, f32[96,384]{1,0:T(8,128)}, u32[]{:S(2)}) copy-start(f32[96,384]{1,0:T(8,128)} %param.21) | copy-start | bytes 442372
  14.8 3.7 %copy-start.12 = (f32[96,96]{1,0:T(8,128)S(1)}, f32[96,96]{1,0:T(8,128)}, u32[]{:S(2)}) copy-start(f32[96,96]{1,0:T(8,128)} %param.20) | copy-start | bytes 110596
  14.8 3.7 %copy-start.13 = (f32[96,128]{1,0:T(8,128)S(1)}, f32[96,128]{1,0:T(8,128)}, u32[]{:S(2)}) copy-start(f32[96,128]{1,0:T(8,128)} %param.23) | copy-start | bytes 147460
  14.8 3.7 %copy-start.14 = (f32[96,128]{1,0:T(8,128)S(1)}, f32[96,128]{1,0:T(8,128)}, u32[]{:S(2)}) copy-start(f32[96,128]{1,0:T(8,128)} %param.22) | copy-start | bytes 147460
  14.8 3.7 %copy-start.18 = (s32[1,128]{1,0:T(1,128)S(1)}, s32[1,128]{1,0:T(1,128)}, u32[]{:S(2)}) copy-start(s32[1,128]{1,0:T(1,128)} %param.19) | copy-start | bytes 1540
  14.8 15.1 %all-to-all-start.2 = ((f32[4,96,640]{2,1,0:T(8,128)}), f32[4,96,640]{2,1,0:T(8,128)S(1)}, u32[]{:S(2)}, u32[]{:S(2)}) async-start(f32[4,96,640]{2,1,0:T(8,128)} %broadcast_in_dim.29), calls=%async_computation.2 | async-start | bytes 1966080 | tf_op jit(solution)/shard_map/all_to_all | solution.py:28
  31.0 18.2 %all-to-all-start = ((f32[4,96,736]{2,1,0:T(8,128)}), f32[4,96,736]{2,1,0:T(8,128)S(1)}, u32[]{:S(2)}, u32[]{:S(2)}) async-start(f32[4,96,736]{2,1,0:T(8,128)} %broadcast_in_dim.28), calls=%async_computation | async-start | bytes 2359296 | tf_op jit(solution)/shard_map/all_to_all | solution.py:28
  35.4 9.0 %collective-permute-start = (f32[128,64]{0,1:T(8,128)S(1)}, f32[128,64]{0,1:T(8,128)S(1)}, u32[]{:S(2)}, u32[]{:S(2)}) collective-permute-start(f32[128,64]{0,1:T(8,128)S(1)} %copy.35), channel_id=1, source_target_pairs={{0,4},{4,8},{8,12},{12,16},{16,20},{20,24},{24,28},{28,32},{32,36}... | collective-permute-start | bytes 98312 | tf_op jit(solution)/shard_map/ppermute | solution.py:37
  42.3 5.5 %collective-permute-start.1 = (f32[128,64]{0,1:T(8,128)S(1)}, f32[128,64]{0,1:T(8,128)S(1)}, u32[]{:S(2)}, u32[]{:S(2)}) collective-permute-start(f32[128,64]{0,1:T(8,128)S(1)} %copy.35), channel_id=1, source_target_pairs={{4,0},{8,4},{12,8},{16,12},{20,16},{24,20},{28,24},{32,28},{36,32}... | collective-permute-start | bytes 98312 | tf_op jit(solution)/shard_map/ppermute | solution.py:38
  50.3 9.7 %collective-permute-start.2 = (f32[128,128]{1,0:T(8,128)S(1)}, f32[128,128]{1,0:T(8,128)S(1)}, u32[]{:S(2)}, u32[]{:S(2)}) collective-permute-start(f32[128,128]{1,0:T(8,128)S(1)} %gather_fusion.1), channel_id=1, source_target_pairs={{0,4},{4,8},{8,12},{12,16},{16,20},{20,24},{24,28},{28,32},{32,36}... | collective-permute-start | bytes 196616 | tf_op jit(solution)/shard_map/ppermute | solution.py:37
  56.9 5.6 %collective-permute-start.3 = (f32[128,128]{1,0:T(8,128)S(1)}, f32[128,128]{1,0:T(8,128)S(1)}, u32[]{:S(2)}, u32[]{:S(2)}) collective-permute-start(f32[128,128]{1,0:T(8,128)S(1)} %gather_fusion.1), channel_id=1, source_target_pairs={{4,0},{8,4},{12,8},{16,12},{20,16},{24,20},{28,24},{32,28},{36,32}... | collective-permute-start | bytes 196616 | tf_op jit(solution)/shard_map/ppermute | solution.py:38
  63.6 0.9 copy-start.5
  64.8 0.9 copy-start.3
  70.2 24.0 %all-to-all-start.3 = ((f32[8,312,128]{2,1,0:T(8,128)}), f32[8,312,128]{2,1,0:T(8,128)S(1)}, u32[]{:S(2)}, u32[]{:S(2)}) async-start(f32[8,312,128]{2,1,0:T(8,128)} %broadcast_dynamic-update-slice_fusion.1), calls=%async_computation.3 | async-start | bytes 2555904 | tf_op jit(solution)/shard_map/all_to_all | solution.py:28
  94.2 1.1 copy-start.1
  130.6 1.4 copy-start.2
  131.9 27.0 %all-to-all-start.5 = ((f32[8,8,48,128]{3,2,1,0:T(8,128)}), f32[8,8,48,128]{3,2,1,0:T(8,128)S(1)}, u32[]{:S(2)}, u32[]{:S(2)}) async-start(f32[8,8,48,128]{3,2,1,0:T(8,128)} %broadcast_in_dim.33), calls=%async_computation.5 | async-start | bytes 3145728 | tf_op jit(solution)/shard_map/all_to_all | solution.py:28
  158.9 1.2 copy-start
  160.1 17.2 %copy-start.6 = (f32[384,128]{0,1:T(8,128)S(1)}, f32[384,128]{0,1:T(8,128)}, u32[]{:S(2)}) copy-start(f32[384,128]{0,1:T(8,128)} %copy-done.5) | copy-start | bytes 589828
  167.0 10.7 %copy-start.4 = (f32[384,128]{0,1:T(8,128)S(1)}, f32[384,128]{0,1:T(8,128)}, u32[]{:S(2)}) copy-start(f32[384,128]{0,1:T(8,128)} %copy.47) | copy-start | bytes 589828
  167.0 10.3 %all-to-all-start.6 = ((f32[8,48,128]{2,1,0:T(8,128)}), f32[8,48,128]{2,1,0:T(8,128)S(1)}, u32[]{:S(2)}, u32[]{:S(2)}) async-start(f32[8,48,128]{2,1,0:T(8,128)} %get-tuple-element.14), calls=%async_computation.6 | async-start | bytes 393216 | tf_op jit(solution)/shard_map/all_to_all | solution.py:28
  177.8 2.0 %copy-start.17 = (f32[256]{0:T(256)S(1)}, f32[256]{0:T(256)}, u32[]{:S(2)}) copy-start(f32[256]{0:T(256)} %param.15) | copy-start | bytes 3076
  180.7 9.1 %copy-start.7 = (f32[96,256]{1,0:T(8,128)S(1)}, f32[96,256]{1,0:T(8,128)}, u32[]{:S(2)}) copy-start(f32[96,256]{1,0:T(8,128)} %param.13) | copy-start | bytes 294916
  180.7 9.1 %copy-start.8 = (f32[96,256]{1,0:T(8,128)S(1)}, f32[96,256]{1,0:T(8,128)}, u32[]{:S(2)}) copy-start(f32[96,256]{1,0:T(8,128)} %param.14) | copy-start | bytes 294916
  180.7 9.1 %copy-start.11 = (f32[96,256]{1,0:T(8,128)S(1)}, f32[96,256]{1,0:T(8,128)}, u32[]{:S(2)}) copy-start(f32[96,256]{1,0:T(8,128)} %param.12) | copy-start | bytes 294916
